TPU v7x, 128 devices: a whole 4x4x4 slice. The times are simulated.
128 devices in a mesh: dp: 8 (over y, core), mp: 16 (over x, z).
Axes of the slice: x: 4, y: 4, z: 4, core: 2. Of those that a mesh axis runs over, the one named last changes fastest.
Arguments:
- emb_grad: float32 [65536, 7168], P('dp', 'mp'), may hold values from -600 to 600
- mtp_grad: float32 [14336, 7168], P('dp', 'mp'), may hold values from -600 to 600
- emb_groups: int32 [64], replicated, may hold values from 0 to 31
- mtp_groups: int32 [32], replicated, may hold values from 0 to 31
- max_rms: float32 [1], replicated, may hold values from 0.5 to 2
Outputs:
- emb_clipped: bfloat16 [65536, 7168], P(('dp', 'mp'))
- mtp_clipped: bfloat16 [14336, 7168], P('dp', 'mp')
- group_rms: float32 [32], replicated
All inputs are finite; a program needn't handle non-finite values.
Results may differ from a plain program's by a relative error of at most 0.005.
Values may be sent and summed in bfloat16 or wider, within the bound.
No kernel may reach another device: no remote copies, remote signals or barrier semaphores. Data moves between devices by JAX's collectives and lax.ppermute only.
A program may use at most 128 MiB of HBM per device.

v0:
```python
import jax
import jax.numpy as jnp
from jax import lax
from jax.sharding import Mesh
from jax.sharding import PartitionSpec as P

D = 7168
V = 65536
CAT = 14336
EMB_BLK = 1024
MTP_BLK = 448
GROUPS = 32
DP = ("dp_0", "dp_1")
DP_MP = ("dp_0", "dp_1", "mp_0", "mp_1")
MP = ("mp_0", "mp_1")


def one_axis_at_a_time(value, axes):
    for axis in axes:
        value = lax.psum(value, axis)
    return value


def block_squares(gradient, block_rows):
    blocks = gradient.reshape(gradient.shape[0] // block_rows, block_rows, gradient.shape[1])
    return jnp.sum(jnp.square(blocks), axis=(1, 2))


def membership(labels):
    return (labels[:, None] == jnp.arange(GROUPS, dtype=jnp.int32)[None, :]).astype(jnp.float32)


def on_device(emb_grad, mtp_grad, emb_groups, mtp_groups, max_rms):
    shard = lax.axis_index(DP)
    embed_count = emb_grad.shape[0] // EMB_BLK
    head_count = mtp_grad.shape[0] // MTP_BLK
    embed_labels = lax.dynamic_slice_in_dim(emb_groups, shard * embed_count, embed_count)
    head_labels = lax.dynamic_slice_in_dim(mtp_groups, shard * head_count, head_count)
    emb_low = lax.optimization_barrier(emb_grad.astype(jnp.bfloat16))
    partial_value = jnp.sum(
        block_squares(emb_grad, EMB_BLK)[:, None] * membership(embed_labels), axis=0
    )
    partial_value = partial_value + jnp.sum(
        block_squares(mtp_grad, MTP_BLK)[:, None] * membership(head_labels), axis=0
    )
    group_square = one_axis_at_a_time(partial_value, DP_MP)
    group_size = jnp.sum(membership(emb_groups), axis=0) * jnp.float32(EMB_BLK * D) + jnp.sum(
        membership(mtp_groups), axis=0
    ) * jnp.float32(MTP_BLK * D)
    group_rms = jnp.sqrt(group_square / jnp.maximum(group_size, 1.0))
    global_norm = jnp.sqrt(jnp.sum(group_square))
    ceiling = max_rms[0] * jnp.sqrt(jnp.float32((V + CAT) * D))
    factor = ceiling / (global_norm + 1e-06)
    head_output = (mtp_grad * factor).astype(jnp.bfloat16)
    scaled = (emb_low.astype(jnp.float32) * factor).astype(jnp.bfloat16)
    embed_output = lax.all_to_all(scaled, MP, split_axis=0, concat_axis=1, tiled=True)
    return (embed_output, head_output, group_rms)


def solution(mesh):
    torus = Mesh(mesh.devices.reshape(4, 2, 4, 4), ("dp_0", "dp_1", "mp_0", "mp_1"))
    return jax.shard_map(
        on_device,
        mesh=torus,
        in_specs=(P(DP, MP), P(DP, MP), P(), P(), P()),
        out_specs=(P(DP_MP, None), P(DP, MP), P()),
        check_vma=False,
    )
```

profile of v0, /device:TPU:0, one launch (start us, length us, event | category | flops | bytes accessed | tf_op | source)
XLA Modules:
  0.0 171.9 jit_solution(9425515222135174412)
XLA Ops:
  1.3 0.8 convert_reduce_fusion.1
  2.0 0.7 dynamic_slice.6
  2.8 0.7 convert_reduce_fusion
  3.5 0.7 dynamic_slice.7
  4.3 2.2 %multiply_reduce_fusion.1 = f32[1792]{0:T(1024)S(1)} fusion(f32[1792,448]{0,1:T(8,128)} %param.6), kind=kLoop, calls=%fused_computation.4 | loop fusion | flops 1603840 | bytes 3218432 | tf_op jit(solution)/shard_map/reduce_sum | solution.py:26
  6.4 0.1 reduce_sum.82
  6.5 14.2 %multiply_reduce_fusion = (f32[8192]{0:T(1024)S(1)}, bf16[8192,448]{0,1:T(8,128)(2,1)}) fusion(f32[8192,448]{0,1:T(8,128)} %param.5), kind=kLoop, calls=%fused_computation.1 | loop fusion | flops 11001856 | bytes 22052864 | tf_op jit(solution)/shard_map/reduce_sum | solution.py:26
  20.7 0.1 reduce_sum.83
  20.8 0.1 reduce_sum.79
  20.9 0.1 select_reduce_fusion.1
  21.0 0.1 select_reduce_fusion
  21.1 10.9 %psum.28 = f32[32]{0:T(128)S(1)} all-reduce(f32[32]{0:T(128)S(1)} %add.29), channel_id=1, replica_groups=mesh['dp_0'=4,'dp_1'=2,'mp_0'=4,'mp_1'=4] {'dp_0'}, use_global_device_ids=true, to_apply=%region_6.0 | all-reduce | flops 32 | bytes 256 | tf_op jit(solution)/shard_map/psum | solution.py:20
  32.0 2.5 %psum.29 = f32[32]{0:T(128)S(1)} all-reduce(f32[32]{0:T(128)S(1)} %psum.28), channel_id=1, replica_groups=mesh['dp_0'=4,'dp_1'=2,'mp_0'=4,'mp_1'=4] {'dp_1'}, use_global_device_ids=true, to_apply=%region_7.0 | all-reduce | flops 32 | bytes 256 | tf_op jit(solution)/shard_map/psum | solution.py:20
  34.4 10.5 %psum.30 = f32[32]{0:T(128)S(1)} all-reduce(f32[32]{0:T(128)S(1)} %psum.29), channel_id=1, replica_groups=mesh['dp_0'=4,'dp_1'=2,'mp_0'=4,'mp_1'=4] {'mp_0'}, use_global_device_ids=true, to_apply=%region_8.0 | all-reduce | flops 32 | bytes 256 | tf_op jit(solution)/shard_map/psum | solution.py:20
  44.9 11.8 %psum.31 = f32[32]{0:T(128)S(1)} all-reduce(f32[32]{0:T(128)S(1)} %psum.30), channel_id=1, replica_groups=mesh['dp_0'=4,'dp_1'=2,'mp_0'=4,'mp_1'=4] {'mp_1'}, use_global_device_ids=true, to_apply=%region_9.0 | all-reduce | flops 32 | bytes 256 | tf_op jit(solution)/shard_map/psum | solution.py:20
  56.6 1.1 fusion
  58.5 4.9 %multiply_convert_fusion = bf16[8192,448]{0,1:T(8,128)(2,1)S(1)} fusion(bf16[8192,448]{0,1:T(8,128)(2,1)} %get-tuple-element.16, f32[]{:T(128)S(6)} %div.6), kind=kLoop, calls=%fused_computation | loop fusion | flops 11010048 | bytes 14680068 | tf_op jit(solution)/shard_map/convert_element_type | solution.py:55
  63.4 3.9 %copy.18 = bf16[56,16,8,512]{3,2,0,1:T(8,128)(2,1)} copy(bf16[56,16,8,512]{3,2,1,0:T(8,128)(2,1)S(1)} %bitcast.9) | data formatting | bytes 14680064 | tf_op jit(solution)/shard_map/all_to_all | solution.py:56
  67.2 0.0 copy-start
  67.2 5.0 %all-to-all-start = ((bf16[16,512,448]{1,2,0:T(8,128)(2,1)}), bf16[16,512,448]{1,2,0:T(8,128)(2,1)}, u32[]{:S(2)}, u32[]{:S(2)}) async-start(bf16[16,512,448]{1,2,0:T(8,128)(2,1)} %bitcast.8), calls=%async_computation | async-start | bytes 14680064 | tf_op jit(solution)/shard_map/all_to_all | solution.py:56
  72.2 0.0 copy-done
  72.2 1.4 multiply_convert_fusion.1
  73.6 88.4 %all-to-all-done = bf16[16,512,448]{1,2,0:T(8,128)(2,1)} async-done(((bf16[16,512,448]{1,2,0:T(8,128)(2,1)}), bf16[16,512,448]{1,2,0:T(8,128)(2,1)}, u32[]{:S(2)}, u32[]{:S(2)}) %all-to-all-start) | async-done | bytes 7340064 | tf_op jit(solution)/shard_map/all_to_all | solution.py:56
  162.0 9.9 %copy.15 = bf16[512,7168]{1,0:T(8,128)(2,1)} copy(bf16[512,7168]{0,1:T(8,128)(2,1)} %bitcast.2) | data formatting | bytes 14680064
  (2 shorter events, 0.0 us)
Async XLA Ops:
  67.2 5.0 %copy-start = (f32[1792,448]{0,1:T(8,128)S(1)}, f32[1792,448]{0,1:T(8,128)}, u32[]{:S(2)}) copy-start(f32[1792,448]{0,1:T(8,128)} %param.6) | copy-start | bytes 9633796
  67.2 94.8 %all-to-all-start = ((bf16[16,512,448]{1,2,0:T(8,128)(2,1)}), bf16[16,512,448]{1,2,0:T(8,128)(2,1)}, u32[]{:S(2)}, u32[]{:S(2)}) async-start(bf16[16,512,448]{1,2,0:T(8,128)(2,1)} %bitcast.8), calls=%async_computation | async-start | bytes 14680064 | tf_op jit(solution)/shard_map/all_to_all | solution.py:56
where the time goes:
time: 173 us; the launch traced here: 172 us
  waiting for transfers between devices  88.4 us (51%)
  blocking collectives  35.5 us (21%)
  other arithmetic  25.6 us (15%)
  local copies, waits for them, and re-layouts  15.3 us (9%)
  starting transfers between devices  4.95 us (3%)
  between operations  2.06 us (1%)
    all_to_all x1, waiting for transfers between devices, on_device(): lax.all_to_all(scaled, MP, split_axis=0, concat_axis=1, tiled=True)  88.4 us
    psum x4, blocking collectives, one_axis_at_a_time(): value = lax.psum(value, axis)  35.5 us
    reduce_sum x4, other arithmetic, block_squares(): return jnp.sum(jnp.square(blocks), axis=(1, 2))  16.6 us
    unnamed x3, local copies, waits for them, and re-layouts  9.94 us
    all_to_all x1, starting transfers between devices, on_device(): lax.all_to_all(scaled, MP, split_axis=0, concat_axis=1, tiled=True)  4.95 us
    convert_element_type x1, other arithmetic, on_device(): scaled = (emb_low.astype(jnp.float32) * factor).astype(jnp.bfloat16)  4.88 us
    all_to_all x1, local copies, waits for them, and re-layouts, on_device(): lax.all_to_all(scaled, MP, split_axis=0, concat_axis=1, tiled=True)  3.85 us
  transfers between devices with their start and end apart: 1, of which 1 were waited for; matrix products, arithmetic and copies ran while one was open for 1% of the time, Pallas kernels for 0%

commit v1 on v0

--- a/solution.py
+++ b/solution.py
@@ -17,7 +17,7 @@
 
 def one_axis_at_a_time(value, axes):
     for axis in axes:
-        value = lax.psum(value, axis)
+        value = jnp.sum(lax.all_gather(value, axis), axis=0)
     return value
 
 

time: 173 us -> 178 us (1.029)
  local copies, waits for them, and re-layouts: 15.3 us -> 20.1 us
  between operations: 2.06 us -> 4.67 us
    psum x4 -> x0, blocking collectives: 35.5 us -> none  [one_axis_at_a_time(): value = lax.psum(value, axis)]
    unnamed x0 -> x4, blocking collectives: none -> 35.5 us
    unnamed x3 -> x18, local copies, waits for them, and re-layouts: 9.94 us -> 15.6 us
where the time goes in v1:
time: 178 us; the launch traced here: 177 us
  waiting for transfers between devices  87.6 us (49%)
  blocking collectives  35.5 us (20%)
  other arithmetic  24.5 us (14%)
  local copies, waits for them, and re-layouts  20.1 us (11%)
  starting transfers between devices  4.95 us (3%)
  between operations  4.67 us (3%)
    all_to_all x1, waiting for transfers between devices, on_device(): lax.all_to_all(scaled, MP, split_axis=0, concat_axis=1, tiled=True)  87.6 us
    unnamed x4, blocking collectives  35.5 us
    reduce_sum x4, other arithmetic, block_squares(): return jnp.sum(jnp.square(blocks), axis=(1, 2))  16.6 us
    unnamed x18, local copies, waits for them, and re-layouts  15.6 us
    all_to_all x1, starting transfers between devices, on_device(): lax.all_to_all(scaled, MP, split_axis=0, concat_axis=1, tiled=True)  4.95 us
    convert_element_type x1, other arithmetic, on_device(): scaled = (emb_low.astype(jnp.float32) * factor).astype(jnp.bfloat16)  4.88 us
    all_to_all x1, local copies, waits for them, and re-layouts, on_device(): lax.all_to_all(scaled, MP, split_axis=0, concat_axis=1, tiled=True)  3.85 us
  transfers between devices with their start and end apart: 1, of which 1 were waited for; matrix products, arithmetic and copies ran while one was open for 1% of the time, Pallas kernels for 0%

profile of v1, /device:TPU:0, one launch (start us, length us, event | category | flops | bytes accessed | tf_op | source)
XLA Modules:
  0.0 177.3 jit_solution(16916008249992952427)
XLA Ops:
  1.3 1.2 dynamic-slice.3
  2.5 1.2 dynamic-slice.2
  5.1 1.2 dynamic-slice.1
  7.0 1.2 dynamic-slice
  8.9 2.2 %multiply_reduce_fusion.1 = f32[1792]{0:T(1024)S(1)} fusion(f32[1792,448]{0,1:T(8,128)} %param.6), kind=kLoop, calls=%fused_computation.4 | loop fusion | flops 1603840 | bytes 3218432 | tf_op jit(solution)/shard_map/reduce_sum | solution.py:26
  11.1 14.2 %multiply_reduce_fusion = (f32[8192]{0:T(1024)S(1)}, bf16[8192,448]{0,1:T(8,128)(2,1)}) fusion(f32[8192,448]{0,1:T(8,128)} %param.5), kind=kLoop, calls=%fused_computation.1 | loop fusion | flops 11001856 | bytes 22052864 | tf_op jit(solution)/shard_map/reduce_sum | solution.py:26
  25.5 0.1 reduce_sum.119
  25.6 0.1 select_reduce_fusion.1
  25.7 0.1 reduce_sum.115
  25.8 0.1 select_reduce_fusion
  25.9 0.1 add_dynamic-update-slice_fusion
  26.0 10.8 %all-reduce = f32[128]{0:T(128)S(1)} all-reduce(f32[128]{0:T(128)S(1)} %add_dynamic-update-slice_fusion), channel_id=2, replica_groups=mesh['dp_0'=4,'dp_1'=2,'mp_0'=4,'mp_1'=4] {'dp_0'}, use_global_device_ids=true, to_apply=%add | all-reduce | flops 128 | bytes 1024
  36.8 0.1 reshape.33
  36.9 0.2 dynamic-update-slice.1
  37.2 2.4 %all-reduce.1 = f32[64]{0:T(128)S(1)} all-reduce(f32[64]{0:T(128)S(1)} %dynamic-update-slice.1), channel_id=3, replica_groups=mesh['dp_0'=4,'dp_1'=2,'mp_0'=4,'mp_1'=4] {'dp_1'}, use_global_device_ids=true, to_apply=%add.1 | all-reduce | flops 64 | bytes 512
  39.6 0.1 reshape.34
  39.7 0.2 dynamic-update-slice.2
  40.0 10.5 %all-reduce.2 = f32[128]{0:T(128)S(1)} all-reduce(f32[128]{0:T(128)S(1)} %dynamic-update-slice.2), channel_id=4, replica_groups=mesh['dp_0'=4,'dp_1'=2,'mp_0'=4,'mp_1'=4] {'mp_0'}, use_global_device_ids=true, to_apply=%add.2 | all-reduce | flops 128 | bytes 1024
  50.4 0.1 reshape.35
  50.5 0.2 dynamic-update-slice.3
  50.8 11.7 %all-reduce.3 = f32[128]{0:T(128)S(1)} all-reduce(f32[128]{0:T(128)S(1)} %dynamic-update-slice.3), channel_id=5, replica_groups=mesh['dp_0'=4,'dp_1'=2,'mp_0'=4,'mp_1'=4] {'mp_1'}, use_global_device_ids=true, to_apply=%add.3 | all-reduce | flops 128 | bytes 1024
  62.5 0.6 reduce_sum.124
  63.9 4.9 %multiply_convert_fusion = bf16[8192,448]{0,1:T(8,128)(2,1)S(1)} fusion(bf16[8192,448]{0,1:T(8,128)(2,1)} %get-tuple-element.16, f32[]{:T(128)S(6)} %div.6), kind=kLoop, calls=%fused_computation | loop fusion | flops 11010048 | bytes 14680068 | tf_op jit(solution)/shard_map/convert_element_type | solution.py:55
  68.8 3.9 %copy.18 = bf16[56,16,8,512]{3,2,0,1:T(8,128)(2,1)} copy(bf16[56,16,8,512]{3,2,1,0:T(8,128)(2,1)S(1)} %bitcast.13) | data formatting | bytes 14680064 | tf_op jit(solution)/shard_map/all_to_all | solution.py:56
  72.6 5.0 %all-to-all-start = ((bf16[16,512,448]{1,2,0:T(8,128)(2,1)}), bf16[16,512,448]{1,2,0:T(8,128)(2,1)}, u32[]{:S(2)}, u32[]{:S(2)}) async-start(bf16[16,512,448]{1,2,0:T(8,128)(2,1)} %bitcast.12), calls=%async_computation | async-start | bytes 14680064 | tf_op jit(solution)/shard_map/all_to_all | solution.py:56
  77.6 0.1 reshape.36
  77.7 0.1 convert_reduce_fusion.1
  77.8 0.1 convert_reduce_fusion
  77.9 0.5 fusion
  78.4 1.4 multiply_convert_fusion.1
  79.8 87.6 %all-to-all-done = bf16[16,512,448]{1,2,0:T(8,128)(2,1)} async-done(((bf16[16,512,448]{1,2,0:T(8,128)(2,1)}), bf16[16,512,448]{1,2,0:T(8,128)(2,1)}, u32[]{:S(2)}, u32[]{:S(2)}) %all-to-all-start) | async-done | bytes 7340064 | tf_op jit(solution)/shard_map/all_to_all | solution.py:56
  167.4 9.9 %copy.15 = bf16[512,7168]{1,0:T(8,128)(2,1)} copy(bf16[512,7168]{0,1:T(8,128)(2,1)} %bitcast.6) | data formatting | bytes 14680064
  (18 shorter events, 0.4 us)
Async XLA Ops:
  11.1 14.2 %copy-start.1 = (s32[64]{0:T(128)S(1)}, s32[64]{0:T(128)}, u32[]{:S(2)}) copy-start(s32[64]{0:T(128)} %param.7) | copy-start | bytes 772
  11.1 14.3 %copy-start.2 = (s32[32]{0:T(128)S(1)}, s32[32]{0:T(128)}, u32[]{:S(2)}) copy-start(s32[32]{0:T(128)} %param.8) | copy-start | bytes 388
  72.6 5.8 %copy-start = (f32[1792,448]{0,1:T(8,128)S(1)}, f32[1792,448]{0,1:T(8,128)}, u32[]{:S(2)}) copy-start(f32[1792,448]{0,1:T(8,128)} %param.6) | copy-start | bytes 9633796
  72.6 94.8 %all-to-all-start = ((bf16[16,512,448]{1,2,0:T(8,128)(2,1)}), bf16[16,512,448]{1,2,0:T(8,128)(2,1)}, u32[]{:S(2)}, u32[]{:S(2)}) async-start(bf16[16,512,448]{1,2,0:T(8,128)(2,1)} %bitcast.12), calls=%async_computation | async-start | bytes 14680064 | tf_op jit(solution)/shard_map/all_to_all | solution.py:56
